TPU v7x, 512 devices: a whole 4x8x8 slice. The times are simulated.
512 devices in a mesh: dp: 128 (over z, y, core), mp: 4 (over x).
Axes of the slice: x: 4, y: 8, z: 8, core: 2. Of those that a mesh axis runs over, the one named last changes fastest.
Arguments:
- bag_lengths: int32 [16, 16384], P('mp', 'dp'), may hold values from 1 to 8
- owners: int32 [16, 16384, 8, 1], P('mp', 'dp'), may hold values from 0 to 127; in each aligned block of 1024 rows (0 to 1023, 1024 to 2047, ..., all dimensions but the last counted through in order) at most 16 rows name the same one
- row_slots: int32 [16, 16384, 8], P('mp', 'dp'), may hold values from 0 to 511
- admit_mask: int32 [16, 16384, 8], P('mp', 'dp'), may hold values 0 or 1
- expired: int32 [16, 65536], P('mp', 'dp'), may hold values 0 or 1
- embeddings: float32 [16, 65536, 128], P('mp', 'dp'), may hold values from -3 to 3
- accumulator: float32 [16, 65536], P('mp', 'dp'), may hold values from 0.001 to 0.01
- hidden_weight: bfloat16 [2048, 1024], P(None, 'mp'), may hold values from -0.125 to 0.125
- output_weight: float32 [1024], P('mp'), may hold values from -0.9 to 0.9
- labels: int32 [16384], P('dp'), may hold values 0 or 1
Outputs:
- new_table: float32 [16, 65536, 128], P('mp', 'dp')
- new_accum: float32 [16, 65536], P('mp', 'dp')
- weight_grad: bfloat16 [2048, 1024], P(None, 'mp')
- logits: float32 [16384], P('dp')
Inputs may be any that keep to these rules, and one draw needn't show every extreme that they name: Among the 128 x 8 lookups of one index of dp into one table (aligned blocks of owners' rows), at most 16 name the same owner; in some blocks one owner is named exactly 16 times.
All inputs are finite; a program needn't handle non-finite values. No bound on the sum of `admit_mask` or of `expired` or of `labels` on one device may be relied on, other than what follows from the above.
Results may differ from a plain program's by a relative error of at most 0.0085.
Values may be sent and summed in bfloat16 or wider, within the bound.
No kernel may reach another device: no remote copies, remote signals or barrier semaphores. Data moves between devices by JAX's collectives and lax.ppermute only.
A program may use at most 64 MiB of HBM per device.

v0:
```python
import jax
import jax.numpy as jnp
from jax import lax
from jax.sharding import Mesh
from jax.sharding import PartitionSpec as P

DP = ("dp_0", "dp_1", "dp_2")
LEARN_RATE = 0.05
ACC_RESET = 0.001


def joined_along(parts, dim):
    parts = jnp.moveaxis(parts, 0, dim)
    dims = parts.shape
    return parts.reshape(*dims[:dim], dims[dim] * dims[dim + 1], *dims[dim + 2 :])


def from_everyone(value, axis):
    size = lax.axis_size(axis)
    return lax.all_to_all(
        jnp.broadcast_to(value[None], (size, *value.shape)), axis, 0, 0, tiled=True
    )


def collect_2(value, axis, dim):
    return joined_along(from_everyone(value, axis), dim)


def taken_together(value, axis):
    return from_everyone(value, axis).sum(axis=0)


def cut_along(value, dim, size):
    dims = value.shape
    parts = value.reshape(*dims[:dim], size, dims[dim] // size, *dims[dim + 1 :])
    return jnp.moveaxis(parts, dim, 0)


def summed_on_arrival(value, axis, dim):
    parts = cut_along(value, dim, lax.axis_size(axis))
    arrived = lax.all_to_all(parts, axis, split_axis=0, concat_axis=0, tiled=True)
    return arrived.astype(jnp.float32).sum(axis=0)


def sum_in_two_steps(value, axes, dim):
    far, near = axes
    parts = cut_along(value, dim, lax.axis_size(far))
    nearer = summed_on_arrival(parts, near, dim + 1)
    arrived = lax.all_to_all(
        nearer.astype(jnp.bfloat16), far, split_axis=0, concat_axis=0, tiled=True
    )
    return arrived.astype(jnp.float32).sum(axis=0)


def filled_up(lines, size):
    spare = -lines.shape[0] % size
    if not spare:
        return lines
    return jnp.concatenate([lines, jnp.zeros((spare, *lines.shape[1:]), lines.dtype)])


def gathered_by_axis(value, axes, dim):
    far, near = axes
    parts = from_everyone(from_everyone(value, far), near)
    return joined_along(parts.swapaxes(0, 1).reshape(-1, *value.shape), dim)


def sum_by_parts(value, axes):
    lines = value.reshape(-1, value.shape[-1])
    own = sum_in_two_steps(
        filled_up(lines, lax.axis_size(axes[0]) * lax.axis_size(axes[1])), axes, 0
    )
    whole = gathered_by_axis(own.astype(jnp.bfloat16), axes, 0)
    return whole[: len(lines)].reshape(value.shape).astype(jnp.float32)


def silu_slope(preact):
    sig = jax.nn.sigmoid(preact)
    return sig * (1.0 + preact * (1.0 - sig))


def shards(
    bag_lengths,
    owners,
    row_slots,
    admit_mask,
    expired,
    embeddings,
    accumulator,
    hidden_weight,
    output_weight,
    labels,
):
    groups = lax.axis_size(DP)
    tab_dev, tok_dev, bag_size = row_slots.shape
    rows_dev = embeddings.shape[1]
    row_width = embeddings.shape[2]
    lookups = tok_dev * bag_size
    capacity = 2 * lookups // groups
    buffer_len = groups * capacity
    places = jnp.arange(bag_size, dtype=jnp.int32)
    live_mask = ((places[None, None, :] < bag_lengths[:, :, None]) & (admit_mask == 1)).astype(
        jnp.float32
    )
    counted = jnp.sum(live_mask, axis=2)
    bag_weight = live_mask / jnp.maximum(counted, 1.0)[:, :, None]
    target = owners[..., 0].reshape(tab_dev, lookups)
    lookup_ids = jnp.arange(lookups, dtype=jnp.int32)
    earlier = lookup_ids[None, :] < lookup_ids[:, None]
    same_owner = target[:, :, None] == target[:, None, :]
    ranked = jnp.sum((same_owner & earlier[None, :, :]).astype(jnp.int32), axis=2)
    placed = target * capacity + ranked
    slot_ids = jnp.arange(buffer_len, dtype=jnp.int32)
    hits = placed[:, :, None] == slot_ids[None, None, :]
    flat_slots = row_slots.reshape(tab_dev, lookups)
    request = jnp.sum(jnp.where(hits, flat_slots[:, :, None], 0), axis=1)
    sample_of = lookup_ids // bag_size
    slot_sample = jnp.sum(jnp.where(hits, sample_of[None, :, None], 0), axis=1)
    flat_weight = bag_weight.reshape(tab_dev, lookups)
    slot_weight = jnp.sum(jnp.where(hits, flat_weight[:, :, None], jnp.float32(0.0)), axis=1)
    pool_matrix = jnp.sum(
        jnp.where(
            hits.reshape(tab_dev, tok_dev, bag_size, buffer_len),
            bag_weight[:, :, :, None],
            jnp.float32(0.0),
        ),
        axis=2,
    )
    request = request.reshape(tab_dev, groups, capacity)
    arrived = lax.all_to_all(request, DP, split_axis=1, concat_axis=1, tiled=True)
    fresh_rows = jnp.where(expired[:, :, None] == 1, jnp.float32(0.0), embeddings)
    fresh_acc = jnp.where(expired == 1, jnp.float32(ACC_RESET), accumulator)
    row_pick = (
        arrived.reshape(tab_dev, buffer_len)[:, :, None]
        == jnp.arange(rows_dev, dtype=jnp.int32)[None, None, :]
    ).astype(jnp.bfloat16)
    fetched = jnp.einsum(
        "tbr,tre->tbe",
        row_pick,
        fresh_rows.astype(jnp.bfloat16),
        preferred_element_type=jnp.float32,
    ).astype(jnp.bfloat16)
    fetched = fetched.reshape(tab_dev, groups, capacity, row_width)
    returned = lax.all_to_all(fetched, DP, split_axis=1, concat_axis=1, tiled=True)
    returned_rows = returned.reshape(tab_dev, buffer_len, row_width).astype(jnp.float32)
    pooled = jnp.einsum("tnb,tbe->tne", pool_matrix, returned_rows, precision=lax.Precision.HIGHEST)
    features = pooled.transpose(1, 0, 2).reshape(tok_dev, tab_dev * row_width).astype(jnp.bfloat16)
    portion = collect_2(features, "mp", 1)
    summed_pre = jnp.dot(portion, hidden_weight, preferred_element_type=jnp.float32)
    hidden = jax.nn.silu(summed_pre).astype(jnp.bfloat16)
    logits = taken_together(jnp.sum(hidden.astype(jnp.float32) * output_weight, axis=1), "mp")
    dlogit = jax.nn.sigmoid(logits) - labels.astype(jnp.float32)
    dhidden = (dlogit[:, None] * output_weight * silu_slope(summed_pre)).astype(jnp.bfloat16)
    feature_grad = summed_on_arrival(
        lax.dot_general(
            hidden_weight, dhidden, (((1,), (1,)), ((), ())), preferred_element_type=jnp.float32
        ).astype(jnp.bfloat16),
        "mp",
        0,
    )
    per_table = feature_grad.reshape(tab_dev, row_width, tok_dev).transpose(0, 2, 1)
    sample_pick = (
        slot_sample[:, :, None] == jnp.arange(tok_dev, dtype=jnp.int32)[None, None, :]
    ).astype(jnp.float32)
    slot_grad = jnp.einsum("tbn,tne->tbe", sample_pick, per_table, precision=lax.Precision.HIGHEST)
    outgoing = (slot_weight[:, :, None] * slot_grad).astype(jnp.bfloat16)
    outgoing = outgoing.reshape(tab_dev, groups, capacity, row_width)
    grad_part = lax.all_to_all(outgoing, DP, split_axis=1, concat_axis=1, tiled=True)
    slot_part = lax.all_to_all(request, DP, split_axis=1, concat_axis=1, tiled=True)
    items = grad_part.shape[0]
    selector = (
        slot_part.reshape(items, -1)[:, :, None] == jnp.arange(rows_dev, dtype=jnp.int32)
    ).astype(jnp.bfloat16)
    summed = jnp.einsum(
        "ksr,kse->kre",
        selector,
        grad_part.reshape(items, -1, row_width),
        preferred_element_type=jnp.float32,
    )
    new_acc = fresh_acc + jnp.mean(summed * summed, axis=2)
    new_rows = fresh_rows - LEARN_RATE * summed / jnp.sqrt(new_acc)[:, :, None]
    local_grad = lax.dot_general(
        portion, dhidden, (((0,), (0,)), ((), ())), preferred_element_type=jnp.float32
    )
    weight_grad = sum_by_parts(local_grad.astype(jnp.bfloat16), (("dp_0", "dp_1"), "dp_2")).astype(
        jnp.bfloat16
    )
    return (new_rows, new_acc, weight_grad, logits)


def solution(mesh):
    split = Mesh(mesh.devices.reshape(8, 8, 2, mesh.shape["mp"]), ("dp_0", "dp_1", "dp_2", "mp"))
    return jax.shard_map(
        shards,
        mesh=split,
        in_specs=(
            P("mp", DP),
            P("mp", DP, None, None),
            P("mp", DP, None),
            P("mp", DP, None),
            P("mp", DP),
            P("mp", DP, None),
            P("mp", DP),
            P(None, "mp"),
            P("mp"),
            P(DP),
        ),
        out_specs=(P("mp", DP, None), P("mp", DP), P(None, "mp"), P(DP)),
        check_vma=False,
    )
```

profile of v0, /device:TPU:8, one launch (start us, length us, event | category | flops | bytes accessed | tf_op | source)
XLA Modules:
  0.0 286.2 jit_solution(5932102573414470503)
XLA Ops:
  0.7 0.3 iota_compare_fusion.6
  1.0 0.9 copy.95
  2.1 3.6 %convert_reduce_fusion = s32[4,1024]{1,0:T(4,128)S(1)} fusion(s32[4,1024]{1,0:T(4,128)S(1)} %reshape_squeeze.3, pred[1024,1024]{1,0:T(8,128)(4,1)S(1)} %iota_compare_fusion.6), kind=kLoop, calls=%fused_computation.9 | loop fusion | flops 16773120 | bytes 1081344 | tf_op jit(solution)/shard_map/reduce_sum | solution.py:111
  5.7 0.8 copy.96
  6.6 0.2 broadcast_in_dim.76
  6.7 11.5 %select_reduce_fusion.1 = (s32[4,2048]{1,0:T(4,128)S(1)}, s32[4,2048]{1,0:T(4,128)S(1)}) fusion(s32[1024]{0:T(1024)S(1)} %add_select_fusion, s32[4,1024]{1,0:T(4,128)S(1)} %multiply_add_fusion, s32[4,1024]{1,0:T(4,128)S(1)} %broadcast_in_dim.76), kind=kLoop, calls=%fused_computation.2 | loop fusion | flops 41926656 | bytes 102400 | tf_op jit(solution)/shard_map/reduce_sum | solution.py:118
  18.4 0.9 copy.97
  19.3 17.8 %all-to-all-start = ((s32[4,128,16]{2,0,1:T(4,128)}), s32[4,128,16]{2,0,1:T(4,128)}, u32[]{:S(2)}, u32[]{:S(2)}) async-start(s32[4,128,16]{2,0,1:T(4,128)} %copy.97), calls=%async_computation | async-start | bytes 524288 | tf_op jit(solution)/shard_map/all_to_all | solution.py:169
  37.1 0.3 copy.94
  37.5 13.9 %all-to-all-done = s32[4,128,16]{2,0,1:T(4,128)} async-done(((s32[4,128,16]{2,0,1:T(4,128)}), s32[4,128,16]{2,0,1:T(4,128)}, u32[]{:S(2)}, u32[]{:S(2)}) %all-to-all-start) | async-done | bytes 32800 | tf_op jit(solution)/shard_map/all_to_all | solution.py:169
  51.4 1.0 copy.98
  52.5 3.3 %fusion.5 = bf16[4,2048,128]{2,1,0:T(8,128)(2,1)S(1)} fusion(s32[4,2048]{1,0:T(4,128)S(1)} %eq.91, f32[4,512,128]{1,2,0:T(8,128)S(1)} %copy.94, pred[4,512]{1,0:T(4,128)(4,1)S(1)} %broadcast_compare_fusion), kind=kOutput, calls=%fused_computation.16 | convolution fusion | flops 1079246848 | bytes 3180544 | tf_op jit(solution)/shard_map/tbr,tre->tbe/dot_general | solution.py:137
  55.9 2.0 copy.103
  57.9 6.1 %all-to-all-start.1 = ((bf16[4,128,16,128]{3,2,0,1:T(8,128)(2,1)}), bf16[4,128,16,128]{3,2,0,1:T(8,128)(2,1)S(1)}, u32[]{:S(2)}, u32[]{:S(2)}) async-start(bf16[4,128,16,128]{3,2,0,1:T(8,128)(2,1)} %copy.103), calls=%async_computation.1 | async-start | bytes 4194304 | tf_op jit(solution)/shard_map/all_to_all | solution.py:144
  64.0 0.9 reduce_sum.121
  65.1 1.1 bitcast_add_fusion
  66.2 12.9 %select_reduce_fusion = f32[4,128,2048]{2,1,0:T(8,128)} fusion(f32[4,128,8]{2,1,0:T(8,128)S(1)} %copy.99, s32[4,128,8]{2,1,0:T(8,128)S(1)} %bitcast_add_fusion), kind=kLoop, calls=%fused_computation | loop fusion | flops 24117248 | bytes 4227072 | tf_op jit(solution)/shard_map/reduce_sum | solution.py:121
  79.1 39.1 %all-to-all-done.1 = bf16[4,128,16,128]{3,2,0,1:T(8,128)(2,1)S(1)} async-done(((bf16[4,128,16,128]{3,2,0,1:T(8,128)(2,1)}), bf16[4,128,16,128]{3,2,0,1:T(8,128)(2,1)S(1)}, u32[]{:S(2)}, u32[]{:S(2)}) %all-to-all-start.1) | async-done | bytes 2097184 | tf_op jit(solution)/shard_map/all_to_all | solution.py:144
  118.2 0.4 copy.104
  118.5 1.8 copy-done.1
  120.3 2.5 convolution_convert_fusion.2
  122.9 12.9 %all_to_all.52 = bf16[4,128,512]{1,2,0:T(8,128)(2,1)S(1)} all-to-all(bf16[4,128,512]{1,2,0:T(8,128)(2,1)S(1)} %broadcast_in_dim.121), channel_id=1, replica_groups=mesh['dp_0'=8,'dp_1'=8,'dp_2'=2,'mp'=4] {'mp'}, dimensions={0} | all-to-all | bytes 1048576 | tf_op jit(solution)/shard_map/all_to_all | solution.py:20
  135.8 0.4 multiply_reduce_fusion.1
  136.3 7.6 %all_to_all.53 = f32[4,1,128]{2,1,0:T(1,128)S(1)} all-to-all(f32[4,1,128]{2,1,0:T(1,128)S(1)} %broadcast_in_dim.122), channel_id=1, replica_groups=mesh['dp_0'=8,'dp_1'=8,'dp_2'=2,'mp'=4] {'mp'}, dimensions={0} | all-to-all | bytes 4096 | tf_op jit(solution)/shard_map/all_to_all | solution.py:20
  143.9 0.5 convolution_convert_fusion
  144.5 4.6 %all_to_all.54 = bf16[2,64,16,256]{3,2,1,0:T(8,128)(2,1)S(1)} all-to-all(bf16[2,64,16,256]{3,2,1,0:T(8,128)(2,1)S(1)} %bitcast.40), channel_id=1, replica_groups=mesh['dp_0'=8,'dp_1'=8,'dp_2'=2,'mp'=4] {'dp_2'}, dimensions={0} | all-to-all | bytes 2097152 | tf_op jit(solution)/shard_map/all_to_all | solution.py:41
  149.1 1.1 reduce_sum.127
  150.2 6.2 %all-to-all-start.7 = ((bf16[64,16,256]{2,1,0:T(8,128)(2,1)}), bf16[64,16,256]{2,1,0:T(8,128)(2,1)S(1)}, u32[]{:S(2)}, u32[]{:S(2)}) async-start(bf16[64,16,256]{2,1,0:T(8,128)(2,1)} %reduce_sum.127), calls=%async_computation.7 | async-start | bytes 1048576 | tf_op jit(solution)/shard_map/all_to_all | solution.py:49
  156.5 0.5 convolution_convert_fusion.1
  156.9 0.8 copy.125
  157.8 18.2 %all-to-all-done.7 = bf16[64,16,256]{2,1,0:T(8,128)(2,1)S(1)} async-done(((bf16[64,16,256]{2,1,0:T(8,128)(2,1)}), bf16[64,16,256]{2,1,0:T(8,128)(2,1)S(1)}, u32[]{:S(2)}, u32[]{:S(2)}) %all-to-all-start.7) | async-done | bytes 524320 | tf_op jit(solution)/shard_map/all_to_all | solution.py:49
  175.9 3.5 %all-to-all-start.4 = ((bf16[4,512,128]{1,2,0:T(8,128)(2,1)}), bf16[4,512,128]{1,2,0:T(8,128)(2,1)S(1)}, u32[]{:S(2)}, u32[]{:S(2)}) async-start(bf16[4,512,128]{1,2,0:T(8,128)(2,1)} %bitcast.37), calls=%async_computation.4 | async-start | bytes 1048576 | tf_op jit(solution)/shard_map/all_to_all | solution.py:41
  179.7 7.8 %all-to-all-done.4 = bf16[4,512,128]{1,2,0:T(8,128)(2,1)S(1)} async-done(((bf16[4,512,128]{1,2,0:T(8,128)(2,1)}), bf16[4,512,128]{1,2,0:T(8,128)(2,1)S(1)}, u32[]{:S(2)}, u32[]{:S(2)}) %all-to-all-start.4) | async-done | bytes 524320 | tf_op jit(solution)/shard_map/all_to_all | solution.py:41
  187.5 0.8 broadcast_in_dim.124
  188.3 6.7 %all-to-all-start.8 = ((bf16[64,16,256]{2,1,0:T(8,128)(2,1)}), bf16[64,16,256]{2,1,0:T(8,128)(2,1)S(1)}, u32[]{:S(2)}, u32[]{:S(2)}) async-start(bf16[64,16,256]{2,1,0:T(8,128)(2,1)} %broadcast_in_dim.124), calls=%async_computation.8 | async-start | bytes 1048576 | tf_op jit(solution)/shard_map/all_to_all | solution.py:20
  195.0 4.9 %select_reduce_fusion.2 = f32[4,2048]{1,0:T(4,128)S(1)} fusion(f32[4,1024]{1,0:T(4,128)S(1)} %broadcast_in_dim.115, s32[4,1024]{1,0:T(4,128)S(1)} %multiply_add_fusion), kind=kLoop, calls=%fused_computation.3 | loop fusion | flops 25157632 | bytes 65536 | tf_op jit(solution)/shard_map/reduce_sum | solution.py:120
  200.2 3.8 %multiply_convert_fusion = bf16[4,2048,128]{2,1,0:T(8,128)(2,1)S(1)} fusion(f32[4,128,128]{2,1,0:T(8,128)S(1)} %bitcast.49, s32[4,2048]{1,0:T(4,128)S(1)} %get-tuple-element.28, f32[4,2048]{1,0:T(4,128)S(1)} %select_reduce_fusion.2), kind=kOutput, calls=%fused_computation.12 | convolution fusion | flops 1613758464 | bytes 2424832 | tf_op jit(solution)/shard_map/tbn,tne->tbe/dot_general | solution.py:165
  204.0 2.0 copy.110
  206.0 7.5 %all-to-all-done.8 = bf16[64,16,256]{2,1,0:T(8,128)(2,1)S(1)} async-done(((bf16[64,16,256]{2,1,0:T(8,128)(2,1)}), bf16[64,16,256]{2,1,0:T(8,128)(2,1)S(1)}, u32[]{:S(2)}, u32[]{:S(2)}) %all-to-all-start.8) | async-done | bytes 524320 | tf_op jit(solution)/shard_map/all_to_all | solution.py:20
  213.5 5.4 %all_to_all.55 = bf16[2,64,16,256]{3,2,1,0:T(8,128)(2,1)} all-to-all(bf16[2,64,16,256]{3,2,1,0:T(8,128)(2,1)S(1)} %broadcast_in_dim.125), channel_id=1, replica_groups=mesh['dp_0'=8,'dp_1'=8,'dp_2'=2,'mp'=4] {'dp_2'}, dimensions={0} | all-to-all | bytes 2097152 | tf_op jit(solution)/shard_map/all_to_all | solution.py:20
  218.9 6.1 %all-to-all-start.5 = ((bf16[4,128,16,128]{3,2,0,1:T(8,128)(2,1)}), bf16[4,128,16,128]{3,2,0,1:T(8,128)(2,1)S(1)}, u32[]{:S(2)}, u32[]{:S(2)}) async-start(bf16[4,128,16,128]{3,2,0,1:T(8,128)(2,1)} %copy.110), calls=%async_computation.5 | async-start | bytes 4194304 | tf_op jit(solution)/shard_map/all_to_all | solution.py:168
  225.1 2.3 copy.114
  227.4 51.8 %all-to-all-done.5 = bf16[4,128,16,128]{3,2,0,1:T(8,128)(2,1)S(1)} async-done(((bf16[4,128,16,128]{3,2,0,1:T(8,128)(2,1)}), bf16[4,128,16,128]{3,2,0,1:T(8,128)(2,1)S(1)}, u32[]{:S(2)}, u32[]{:S(2)}) %all-to-all-start.5) | async-done | bytes 2097184 | tf_op jit(solution)/shard_map/all_to_all | solution.py:168
  279.2 0.4 copy.111
  279.6 4.4 %multiply_reduce_fusion = (f32[4,512]{1,0:T(4,128)S(1)}, f32[4,512,128]{1,2,0:T(8,128)S(1)}) fusion(bf16[4,2048,128]{2,1,0:T(8,128)(2,1)S(1)} %bitcast.41, s32[4,2048]{1,0:T(4,128)S(1)} %eq.91), kind=kOutput, calls=%fused_computation.23 | convolution fusion | flops 1078458368 | bytes 3186688 | tf_op jit(solution)/shard_map/ksr,kse->kre/dot_general | solution.py:174
  284.0 0.6 fusion.14
  284.6 0.3 divide_subtract_fusion
  284.9 1.3 copy.115
  (45 shorter events, 1.4 us)
Async XLA Ops:
  0.6 135.2 %copy-start = (bf16[2048,256]{1,0:T(8,128)(2,1)S(1)}, bf16[2048,256]{1,0:T(8,128)(2,1)}, u32[]{:S(2)}) copy-start(bf16[2048,256]{1,0:T(8,128)(2,1)} %param.17) | copy-start | bytes 3145732
  0.6 36.4 %copy-start.6 = (s32[4,512]{1,0:T(4,128)S(1)}, s32[4,512]{1,0:T(4,128)}, u32[]{:S(2)}) copy-start(s32[4,512]{1,0:T(4,128)} %param.14) | copy-start | bytes 24580
  0.7 36.5 %copy-start.5 = (f32[4,512,128]{2,1,0:T(8,128)S(1)}, f32[4,512,128]{2,1,0:T(8,128)}, u32[]{:S(2)}) copy-start(f32[4,512,128]{2,1,0:T(8,128)} %param.15) | copy-start | bytes 3145732
  1.9 53.9 %copy-start.4 = (s32[4,128,8,1]{2,1,0,3:T(8,128)}, s32[4,128,8,1]{2,1,0,3:T(8,128)S(1)}, u32[]{:S(2)}) copy-start(s32[4,128,8,1]{2,1,0,3:T(8,128)S(1)} %copy.95) | copy-start | bytes 49156
  19.3 32.2 %all-to-all-start = ((s32[4,128,16]{2,0,1:T(4,128)}), s32[4,128,16]{2,0,1:T(4,128)}, u32[]{:S(2)}, u32[]{:S(2)}) async-start(s32[4,128,16]{2,0,1:T(4,128)} %copy.97), calls=%async_computation | async-start | bytes 524288 | tf_op jit(solution)/shard_map/all_to_all | solution.py:169
  37.5 18.4 %copy-start.2 = (f32[4,512,128]{1,2,0:T(8,128)}, f32[4,512,128]{1,2,0:T(8,128)S(1)}, u32[]{:S(2)}) copy-start(f32[4,512,128]{1,2,0:T(8,128)S(1)} %copy.94) | copy-start | bytes 3145732
  55.9 9.0 %copy-start.7 = (s32[4,128,8]{1,2,0:T(8,128)S(1)}, s32[4,128,8]{1,2,0:T(8,128)}, u32[]{:S(2)}) copy-start(s32[4,128,8]{1,2,0:T(8,128)} %param.13) | copy-start | bytes 49156
  55.9 9.0 %copy-start.10 = (s32[4,128]{1,0:T(4,128)S(1)}, s32[4,128]{1,0:T(4,128)}, u32[]{:S(2)}) copy-start(s32[4,128]{1,0:T(4,128)} %param.10) | copy-start | bytes 6148
  57.9 60.3 %all-to-all-start.1 = ((bf16[4,128,16,128]{3,2,0,1:T(8,128)(2,1)}), bf16[4,128,16,128]{3,2,0,1:T(8,128)(2,1)S(1)}, u32[]{:S(2)}, u32[]{:S(2)}) async-start(bf16[4,128,16,128]{3,2,0,1:T(8,128)(2,1)} %copy.103), calls=%async_computation.1 | async-start | bytes 4194304 | tf_op jit(solution)/shard_map/all_to_all | solution.py:144
  118.2 2.2 copy-start.1
  118.5 17.3 %copy-start.9 = (f32[256]{0:T(256)S(1)}, f32[256]{0:T(256)}, u32[]{:S(2)}) copy-start(f32[256]{0:T(256)} %param.18) | copy-start | bytes 3076
  120.3 23.6 %copy-start.12 = (s32[128]{0:T(128)S(1)}, s32[128]{0:T(128)}, u32[]{:S(2)}) copy-start(s32[128]{0:T(128)} %param.19) | copy-start | bytes 1540
  143.9 6.3 %copy-start.11 = (f32[128]{0:T(128)}, f32[128]{0:T(128)S(1)}, u32[]{:S(2)}) copy-start(f32[128]{0:T(128)S(1)} %reduce_sum.124) | copy-start | bytes 1540
  150.2 25.7 %all-to-all-start.7 = ((bf16[64,16,256]{2,1,0:T(8,128)(2,1)}), bf16[64,16,256]{2,1,0:T(8,128)(2,1)S(1)}, u32[]{:S(2)}, u32[]{:S(2)}) async-start(bf16[64,16,256]{2,1,0:T(8,128)(2,1)} %reduce_sum.127), calls=%async_computation.7 | async-start | bytes 1048576 | tf_op jit(solution)/shard_map/all_to_all | solution.py:49
  175.9 11.5 %all-to-all-start.4 = ((bf16[4,512,128]{1,2,0:T(8,128)(2,1)}), bf16[4,512,128]{1,2,0:T(8,128)(2,1)S(1)}, u32[]{:S(2)}, u32[]{:S(2)}) async-start(bf16[4,512,128]{1,2,0:T(8,128)(2,1)} %bitcast.37), calls=%async_computation.4 | async-start | bytes 1048576 | tf_op jit(solution)/shard_map/all_to_all | solution.py:41
  188.3 25.2 %all-to-all-start.8 = ((bf16[64,16,256]{2,1,0:T(8,128)(2,1)}), bf16[64,16,256]{2,1,0:T(8,128)(2,1)S(1)}, u32[]{:S(2)}, u32[]{:S(2)}) async-start(bf16[64,16,256]{2,1,0:T(8,128)(2,1)} %broadcast_in_dim.124), calls=%async_computation.8 | async-start | bytes 1048576 | tf_op jit(solution)/shard_map/all_to_all | solution.py:20
  218.9 60.3 %all-to-all-start.5 = ((bf16[4,128,16,128]{3,2,0,1:T(8,128)(2,1)}), bf16[4,128,16,128]{3,2,0,1:T(8,128)(2,1)S(1)}, u32[]{:S(2)}, u32[]{:S(2)}) async-start(bf16[4,128,16,128]{3,2,0,1:T(8,128)(2,1)} %copy.110), calls=%async_computation.5 | async-start | bytes 4194304 | tf_op jit(solution)/shard_map/all_to_all | solution.py:168
  279.6 4.4 %copy-start.8 = (f32[4,512]{1,0:T(4,128)S(1)}, f32[4,512]{1,0:T(4,128)}, u32[]{:S(2)}) copy-start(f32[4,512]{1,0:T(4,128)} %param.16) | copy-start | bytes 24580
  279.6 5.0 %copy-start.3 = (f32[4,512,128]{1,2,0:T(8,128)S(1)}, f32[4,512,128]{1,2,0:T(8,128)}, u32[]{:S(2)}) copy-start(f32[4,512,128]{1,2,0:T(8,128)} %copy-done.2) | copy-start | bytes 3145732
where the time goes:
time: 287 us; the launch traced here: 286 us
  waiting for transfers between devices  138 us (48%)
  starting transfers between devices  46.5 us (16%)
  other arithmetic  36.5 us (13%)
  blocking collectives  30.5 us (11%)
  local copies, waits for them, and re-layouts  18 us (6%)
  matrix products  15.4 us (5%)
    all_to_all x1, waiting for transfers between devices, shards(): lax.all_to_all(outgoing, DP, split_axis=1, concat_axis=1, tiled=True)  51.8 us
    all_to_all x1, waiting for transfers between devices, shards(): lax.all_to_all(fetched, DP, split_axis=1, concat_axis=1, tiled=True)  39.1 us
    all_to_all x3, blocking collectives, from_everyone(): lax.all_to_all(jnp.broadcast_to(value[None], (size, *value.shape)), axis,...  25.9 us
    all_to_all x1, waiting for transfers between devices, sum_in_two_steps(): lax.all_to_all(nearer.astype(jnp.bfloat16), far, split_axis=0, concat_axi...  18.2 us
    all_to_all x1, starting transfers between devices, shards(): lax.all_to_all(request, DP, split_axis=1, concat_axis=1, tiled=True)  17.8 us
    all_to_all x1, waiting for transfers between devices, shards(): lax.all_to_all(request, DP, split_axis=1, concat_axis=1, tiled=True)  13.9 us
    reduce_sum x1, other arithmetic, shards(): jnp.sum(jnp.where(hits.reshape(tab_dev, tok_dev, bag_size, buffer_len), b...  12.9 us
    reduce_sum x1, other arithmetic, shards(): slot_sample = jnp.sum(jnp.where(hits, sample_of[None, :, None], 0), axis=1)  11.5 us
  transfers between devices with their start and end apart: 6, of which 6 were waited for; matrix products, arithmetic and copies ran while one was open for 11% of the time, Pallas kernels for 0%

commit v1 on v0

--- a/solution.py
+++ b/solution.py
@@ -141,7 +141,10 @@
         preferred_element_type=jnp.float32,
     ).astype(jnp.bfloat16)
     fetched = fetched.reshape(tab_dev, groups, capacity, row_width)
-    returned = lax.all_to_all(fetched, DP, split_axis=1, concat_axis=1, tiled=True)
+    peers = lax.axis_size(DP)
+    pieces = jnp.stack(jnp.split(fetched, peers, axis=1), axis=0)
+    pieces = lax.all_to_all(pieces, DP, split_axis=0, concat_axis=0)
+    returned = jnp.concatenate(pieces, axis=1)
     returned_rows = returned.reshape(tab_dev, buffer_len, row_width).astype(jnp.float32)
     pooled = jnp.einsum("tnb,tbe->tne", pool_matrix, returned_rows, precision=lax.Precision.HIGHEST)
     features = pooled.transpose(1, 0, 2).reshape(tok_dev, tab_dev * row_width).astype(jnp.bfloat16)

time: 287 us -> 362 us (1.26)
  local copies, waits for them, and re-layouts: 18 us -> 92.9 us
    unnamed x30 -> x159, local copies, waits for them, and re-layouts: 5.29 us -> 80.9 us
  transfers between devices with their start and end apart: 6 -> 6, of which waited for: 6 -> 6; matrix products, arithmetic and copies ran while one was open for 11% -> 9% of each run, Pallas kernels for 0% -> 0%
where the time goes in v1:
time: 362 us; the launch traced here: 361 us
  waiting for transfers between devices  136 us (38%)
  local copies, waits for them, and re-layouts  92.9 us (26%)
  starting transfers between devices  46.7 us (13%)
  other arithmetic  37.8 us (10%)
  blocking collectives  30.5 us (8%)
  matrix products  15.4 us (4%)
    unnamed x159, local copies, waits for them, and re-layouts  80.9 us
    all_to_all x1, waiting for transfers between devices, shards(): lax.all_to_all(outgoing, DP, split_axis=1, concat_axis=1, tiled=True)  51.8 us
    all_to_all x1, waiting for transfers between devices, shards(): pieces = lax.all_to_all(pieces, DP, split_axis=0, concat_axis=0)  37.1 us
    all_to_all x3, blocking collectives, from_everyone(): lax.all_to_all(jnp.broadcast_to(value[None], (size, *value.shape)), axis,...  25.9 us
    all_to_all x1, waiting for transfers between devices, sum_in_two_steps(): lax.all_to_all(nearer.astype(jnp.bfloat16), far, split_axis=0, concat_axi...  18.2 us
    all_to_all x1, starting transfers between devices, shards(): lax.all_to_all(request, DP, split_axis=1, concat_axis=1, tiled=True)  17.8 us
    reduce_sum x1, other arithmetic, shards(): jnp.sum(jnp.where(hits.reshape(tab_dev, tok_dev, bag_size, buffer_len), b...  14.2 us
    all_to_all x1, waiting for transfers between devices, shards(): lax.all_to_all(request, DP, split_axis=1, concat_axis=1, tiled=True)  13.9 us
  transfers between devices with their start and end apart: 6, of which 6 were waited for; matrix products, arithmetic and copies ran while one was open for 9% of the time, Pallas kernels for 0%

profile of v1, /device:TPU:8, one launch (start us, length us, event | category | flops | bytes accessed | tf_op | source)
XLA Modules:
  0.0 360.6 jit_solution(16491223548534019653)
XLA Ops:
  1.0 0.9 copy.731
  2.1 3.6 convert_reduce_fusion
  6.0 11.5 %select_reduce_fusion.1 = (s32[4,2048]{1,0:T(4,128)S(1)}, s32[4,2048]{1,0:T(4,128)S(1)}) fusion(s32[1024]{0:T(1024)S(1)} %add_select_fusion, s32[4,1024]{1,0:T(4,128)S(1)} %multiply_add_fusion, s32[4,1024]{1,0:T(4,128)S(1)} %broadcast_in_dim.76), kind=kLoop, calls=%fused_computation.2 | loop fusion | flops 41926656 | bytes 102400 | tf_op jit(solution)/shard_map/reduce_sum | solution.py:118
  17.7 0.9 copy.733
  18.6 17.8 %all-to-all-start = ((s32[4,128,16]{2,0,1:T(4,128)}), s32[4,128,16]{2,0,1:T(4,128)}, u32[]{:S(2)}, u32[]{:S(2)}) async-start(s32[4,128,16]{2,0,1:T(4,128)} %copy.733), calls=%async_computation | async-start | bytes 524288 | tf_op jit(solution)/shard_map/all_to_all | solution.py:172
  36.8 13.9 %all-to-all-done = s32[4,128,16]{2,0,1:T(4,128)} async-done(((s32[4,128,16]{2,0,1:T(4,128)}), s32[4,128,16]{2,0,1:T(4,128)}, u32[]{:S(2)}, u32[]{:S(2)}) %all-to-all-start) | async-done | bytes 32800 | tf_op jit(solution)/shard_map/all_to_all | solution.py:172
  50.7 1.0 copy.734
  51.8 3.3 fusion.5
  56.4 0.6 constant_dynamic-update-slice_fusion.125
  78.6 0.6 constant_dynamic-update-slice_fusion.88
  87.6 0.6 constant_dynamic-update-slice_fusion.73
  94.9 0.6 constant_dynamic-update-slice_fusion.61
  95.5 0.6 constant_dynamic-update-slice_fusion.60
  105.1 0.6 constant_dynamic-update-slice_fusion.44
  108.1 0.6 constant_dynamic-update-slice_fusion.39
  112.3 0.6 constant_dynamic-update-slice_fusion.32
  114.7 0.6 constant_dynamic-update-slice_fusion.28
  118.9 0.6 constant_dynamic-update-slice_fusion.21
  124.4 0.6 constant_dynamic-update-slice_fusion.12
  132.2 6.3 %all-to-all-start.1 = ((bf16[128,4,1,16,128]{4,3,1,2,0:T(8,128)(2,1)}), bf16[128,4,1,16,128]{4,3,1,2,0:T(8,128)(2,1)S(1)}, u32[]{:S(2)}, u32[]{:S(2)}) async-start(bf16[128,4,1,16,128]{4,3,1,2,0:T(8,128)(2,1)} %constant_dynamic-update-slice_fusion), calls=%async_computation.1 | async-start | bytes 4194304 | tf_op jit(solution)/shard_map/all_to_all | solution.py:146
  138.5 0.9 reduce_sum.121
  139.4 0.8 copy.735
  140.2 1.0 bitcast_add_fusion
  141.2 14.2 %select_reduce_fusion = f32[4,128,2048]{2,1,0:T(8,128)} fusion(f32[4,128,8]{2,1,0:T(8,128)} %copy.735, s32[4,128,8]{2,1,0:T(8,128)S(1)} %bitcast_add_fusion), kind=kLoop, calls=%fused_computation | loop fusion | flops 24117248 | bytes 4227072 | tf_op jit(solution)/shard_map/reduce_sum | solution.py:121
  155.4 37.1 %all-to-all-done.1 = bf16[128,4,1,16,128]{4,3,1,2,0:T(8,128)(2,1)S(1)} async-done(((bf16[128,4,1,16,128]{4,3,1,2,0:T(8,128)(2,1)}), bf16[128,4,1,16,128]{4,3,1,2,0:T(8,128)(2,1)S(1)}, u32[]{:S(2)}, u32[]{:S(2)}) %all-to-all-start.1) | async-done | bytes 2097184 | tf_op jit(solution)/shard_map/all_to_all | solution.py:146
  192.9 1.8 copy-done.1
  194.8 2.5 convolution_convert_fusion.2
  197.4 12.9 %all_to_all.52 = bf16[4,128,512]{1,2,0:T(8,128)(2,1)S(1)} all-to-all(bf16[4,128,512]{1,2,0:T(8,128)(2,1)S(1)} %broadcast_in_dim.121), channel_id=1, replica_groups=mesh['dp_0'=8,'dp_1'=8,'dp_2'=2,'mp'=4] {'mp'}, dimensions={0} | all-to-all | bytes 1048576 | tf_op jit(solution)/shard_map/all_to_all | solution.py:20
  210.7 7.6 %all_to_all.53 = f32[4,1,128]{2,1,0:T(1,128)S(1)} all-to-all(f32[4,1,128]{2,1,0:T(1,128)S(1)} %broadcast_in_dim.122), channel_id=1, replica_groups=mesh['dp_0'=8,'dp_1'=8,'dp_2'=2,'mp'=4] {'mp'}, dimensions={0} | all-to-all | bytes 4096 | tf_op jit(solution)/shard_map/all_to_all | solution.py:20
  219.0 4.6 %all_to_all.54 = bf16[2,64,16,256]{3,2,1,0:T(8,128)(2,1)S(1)} all-to-all(bf16[2,64,16,256]{3,2,1,0:T(8,128)(2,1)S(1)} %bitcast.810), channel_id=1, replica_groups=mesh['dp_0'=8,'dp_1'=8,'dp_2'=2,'mp'=4] {'dp_2'}, dimensions={0} | all-to-all | bytes 2097152 | tf_op jit(solution)/shard_map/all_to_all | solution.py:41
  223.5 1.1 reduce_sum.127
  224.6 6.3 %all-to-all-start.7 = ((bf16[64,16,256]{2,1,0:T(8,128)(2,1)}), bf16[64,16,256]{2,1,0:T(8,128)(2,1)S(1)}, u32[]{:S(2)}, u32[]{:S(2)}) async-start(bf16[64,16,256]{2,1,0:T(8,128)(2,1)} %reduce_sum.127), calls=%async_computation.7 | async-start | bytes 1048576 | tf_op jit(solution)/shard_map/all_to_all | solution.py:49
  231.4 0.8 copy.1016
  232.2 18.2 %all-to-all-done.7 = bf16[64,16,256]{2,1,0:T(8,128)(2,1)S(1)} async-done(((bf16[64,16,256]{2,1,0:T(8,128)(2,1)}), bf16[64,16,256]{2,1,0:T(8,128)(2,1)S(1)}, u32[]{:S(2)}, u32[]{:S(2)}) %all-to-all-start.7) | async-done | bytes 524320 | tf_op jit(solution)/shard_map/all_to_all | solution.py:49
  250.4 3.5 all-to-all-start.4
  254.1 7.8 %all-to-all-done.4 = bf16[4,512,128]{1,2,0:T(8,128)(2,1)S(1)} async-done(((bf16[4,512,128]{1,2,0:T(8,128)(2,1)}), bf16[4,512,128]{1,2,0:T(8,128)(2,1)S(1)}, u32[]{:S(2)}, u32[]{:S(2)}) %all-to-all-start.4) | async-done | bytes 524320 | tf_op jit(solution)/shard_map/all_to_all | solution.py:41
  261.9 0.8 broadcast_in_dim.124
  262.7 6.7 %all-to-all-start.8 = ((bf16[64,16,256]{2,1,0:T(8,128)(2,1)}), bf16[64,16,256]{2,1,0:T(8,128)(2,1)S(1)}, u32[]{:S(2)}, u32[]{:S(2)}) async-start(bf16[64,16,256]{2,1,0:T(8,128)(2,1)} %broadcast_in_dim.124), calls=%async_computation.8 | async-start | bytes 1048576 | tf_op jit(solution)/shard_map/all_to_all | solution.py:20
  269.5 4.9 %select_reduce_fusion.2 = f32[4,2048]{1,0:T(4,128)S(1)} fusion(f32[4,1024]{1,0:T(4,128)S(1)} %broadcast_in_dim.115, s32[4,1024]{1,0:T(4,128)S(1)} %multiply_add_fusion), kind=kLoop, calls=%fused_computation.3 | loop fusion | flops 25157632 | bytes 65536 | tf_op jit(solution)/shard_map/reduce_sum | solution.py:120
  274.6 3.8 %multiply_convert_fusion = bf16[4,2048,128]{2,1,0:T(8,128)(2,1)S(1)} fusion(f32[4,128,128]{2,1,0:T(8,128)S(1)} %bitcast.946, s32[4,2048]{1,0:T(4,128)S(1)} %get-tuple-element.28, f32[4,2048]{1,0:T(4,128)S(1)} %select_reduce_fusion.2), kind=kOutput, calls=%fused_computation.12 | convolution fusion | flops 1613758464 | bytes 2424832 | tf_op jit(solution)/shard_map/tbn,tne->tbe/dot_general | solution.py:168
  278.4 2.0 copy.873
  280.4 7.5 %all-to-all-done.8 = bf16[64,16,256]{2,1,0:T(8,128)(2,1)S(1)} async-done(((bf16[64,16,256]{2,1,0:T(8,128)(2,1)}), bf16[64,16,256]{2,1,0:T(8,128)(2,1)S(1)}, u32[]{:S(2)}, u32[]{:S(2)}) %all-to-all-start.8) | async-done | bytes 524320 | tf_op jit(solution)/shard_map/all_to_all | solution.py:20
  288.0 5.4 %all_to_all.55 = bf16[2,64,16,256]{3,2,1,0:T(8,128)(2,1)} all-to-all(bf16[2,64,16,256]{3,2,1,0:T(8,128)(2,1)S(1)} %broadcast_in_dim.125), channel_id=1, replica_groups=mesh['dp_0'=8,'dp_1'=8,'dp_2'=2,'mp'=4] {'dp_2'}, dimensions={0} | all-to-all | bytes 2097152 | tf_op jit(solution)/shard_map/all_to_all | solution.py:20
  293.3 6.1 %all-to-all-start.5 = ((bf16[4,128,16,128]{3,2,0,1:T(8,128)(2,1)}), bf16[4,128,16,128]{3,2,0,1:T(8,128)(2,1)S(1)}, u32[]{:S(2)}, u32[]{:S(2)}) async-start(bf16[4,128,16,128]{3,2,0,1:T(8,128)(2,1)} %copy.873), calls=%async_computation.5 | async-start | bytes 4194304 | tf_op jit(solution)/shard_map/all_to_all | solution.py:171
  299.5 2.3 copy.877
  301.8 51.8 %all-to-all-done.5 = bf16[4,128,16,128]{3,2,0,1:T(8,128)(2,1)S(1)} async-done(((bf16[4,128,16,128]{3,2,0,1:T(8,128)(2,1)}), bf16[4,128,16,128]{3,2,0,1:T(8,128)(2,1)S(1)}, u32[]{:S(2)}, u32[]{:S(2)}) %all-to-all-start.5) | async-done | bytes 2097184 | tf_op jit(solution)/shard_map/all_to_all | solution.py:171
  354.0 4.4 %multiply_reduce_fusion = (f32[4,512]{1,0:T(4,128)S(1)}, f32[4,512,128]{1,2,0:T(8,128)S(1)}) fusion(bf16[4,2048,128]{2,1,0:T(8,128)(2,1)S(1)} %bitcast.811, s32[4,2048]{1,0:T(4,128)S(1)} %eq.91), kind=kOutput, calls=%fused_computation.23 | convolution fusion | flops 1078458368 | bytes 3186688 | tf_op jit(solution)/shard_map/ksr,kse->kre/dot_general | solution.py:177
  359.3 1.3 copy.878
  (174 shorter events, 75.4 us)
Async XLA Ops:
  0.6 209.6 %copy-start = (bf16[2048,256]{1,0:T(8,128)(2,1)S(1)}, bf16[2048,256]{1,0:T(8,128)(2,1)}, u32[]{:S(2)}) copy-start(bf16[2048,256]{1,0:T(8,128)(2,1)} %param.17) | copy-start | bytes 3145732
  0.6 5.1 %copy-start.7 = (s32[4,128,8]{1,2,0:T(8,128)S(1)}, s32[4,128,8]{1,2,0:T(8,128)}, u32[]{:S(2)}) copy-start(s32[4,128,8]{1,2,0:T(8,128)} %param.12) | copy-start | bytes 49156
  1.0 35.4 %copy-start.6 = (s32[4,512]{1,0:T(4,128)S(1)}, s32[4,512]{1,0:T(4,128)}, u32[]{:S(2)}) copy-start(s32[4,512]{1,0:T(4,128)} %param.14) | copy-start | bytes 24580
  1.0 35.4 %copy-start.5 = (f32[4,512,128]{2,1,0:T(8,128)S(1)}, f32[4,512,128]{2,1,0:T(8,128)}, u32[]{:S(2)}) copy-start(f32[4,512,128]{2,1,0:T(8,128)} %param.15) | copy-start | bytes 3145732
  18.6 32.2 %all-to-all-start = ((s32[4,128,16]{2,0,1:T(4,128)}), s32[4,128,16]{2,0,1:T(4,128)}, u32[]{:S(2)}, u32[]{:S(2)}) async-start(s32[4,128,16]{2,0,1:T(4,128)} %copy.733), calls=%async_computation | async-start | bytes 524288 | tf_op jit(solution)/shard_map/all_to_all | solution.py:172
  36.8 18.4 %copy-start.2 = (f32[4,512,128]{1,2,0:T(8,128)}, f32[4,512,128]{1,2,0:T(8,128)S(1)}, u32[]{:S(2)}) copy-start(f32[4,512,128]{1,2,0:T(8,128)S(1)} %copy.730) | copy-start | bytes 3145732
  132.2 7.2 %copy-start.8 = (s32[4,128,8]{1,2,0:T(8,128)S(1)}, s32[4,128,8]{1,2,0:T(8,128)}, u32[]{:S(2)}) copy-start(s32[4,128,8]{1,2,0:T(8,128)} %param.13) | copy-start | bytes 49156
  132.2 7.2 %copy-start.11 = (s32[4,128]{1,0:T(4,128)S(1)}, s32[4,128]{1,0:T(4,128)}, u32[]{:S(2)}) copy-start(s32[4,128]{1,0:T(4,128)} %param.10) | copy-start | bytes 6148
  132.2 60.4 %all-to-all-start.1 = ((bf16[128,4,1,16,128]{4,3,1,2,0:T(8,128)(2,1)}), bf16[128,4,1,16,128]{4,3,1,2,0:T(8,128)(2,1)S(1)}, u32[]{:S(2)}, u32[]{:S(2)}) async-start(bf16[128,4,1,16,128]{4,3,1,2,0:T(8,128)(2,1)} %constant_dynamic-update-slice_fusion), calls=%async_computation.1 | async-start | bytes 4194304 | tf_op jit(solution)/shard_map/all_to_all | solution.py:146
  192.6 2.2 copy-start.1
  194.8 15.5 %copy-start.10 = (f32[256]{0:T(256)S(1)}, f32[256]{0:T(256)}, u32[]{:S(2)}) copy-start(f32[256]{0:T(256)} %param.18) | copy-start | bytes 3076
  197.3 21.1 %copy-start.13 = (s32[128]{0:T(128)S(1)}, s32[128]{0:T(128)}, u32[]{:S(2)}) copy-start(s32[128]{0:T(128)} %param.19) | copy-start | bytes 1540
  218.3 5.2 %copy-start.12 = (f32[128]{0:T(128)}, f32[128]{0:T(128)S(1)}, u32[]{:S(2)}) copy-start(f32[128]{0:T(128)S(1)} %reduce_sum.124) | copy-start | bytes 1540
  224.6 25.7 %all-to-all-start.7 = ((bf16[64,16,256]{2,1,0:T(8,128)(2,1)}), bf16[64,16,256]{2,1,0:T(8,128)(2,1)S(1)}, u32[]{:S(2)}, u32[]{:S(2)}) async-start(bf16[64,16,256]{2,1,0:T(8,128)(2,1)} %reduce_sum.127), calls=%async_computation.7 | async-start | bytes 1048576 | tf_op jit(solution)/shard_map/all_to_all | solution.py:49
  230.9 23.0 %copy-start.4 = (f32[4,128,8]{2,1,0:T(8,128)S(1)}, f32[4,128,8]{2,1,0:T(8,128)}, u32[]{:S(2)}) copy-start(f32[4,128,8]{2,1,0:T(8,128)} %copy.735) | copy-start | bytes 49156
  250.4 11.5 %all-to-all-start.4 = ((bf16[4,512,128]{1,2,0:T(8,128)(2,1)}), bf16[4,512,128]{1,2,0:T(8,128)(2,1)S(1)}, u32[]{:S(2)}, u32[]{:S(2)}) async-start(bf16[4,512,128]{1,2,0:T(8,128)(2,1)} %bitcast.807), calls=%async_computation.4 | async-start | bytes 1048576 | tf_op jit(solution)/shard_map/all_to_all | solution.py:41
  262.7 25.2 %all-to-all-start.8 = ((bf16[64,16,256]{2,1,0:T(8,128)(2,1)}), bf16[64,16,256]{2,1,0:T(8,128)(2,1)S(1)}, u32[]{:S(2)}, u32[]{:S(2)}) async-start(bf16[64,16,256]{2,1,0:T(8,128)(2,1)} %broadcast_in_dim.124), calls=%async_computation.8 | async-start | bytes 1048576 | tf_op jit(solution)/shard_map/all_to_all | solution.py:20
  293.3 60.3 %all-to-all-start.5 = ((bf16[4,128,16,128]{3,2,0,1:T(8,128)(2,1)}), bf16[4,128,16,128]{3,2,0,1:T(8,128)(2,1)S(1)}, u32[]{:S(2)}, u32[]{:S(2)}) async-start(bf16[4,128,16,128]{3,2,0,1:T(8,128)(2,1)} %copy.873), calls=%async_computation.5 | async-start | bytes 4194304 | tf_op jit(solution)/shard_map/all_to_all | solution.py:171
  354.0 4.4 %copy-start.9 = (f32[4,512]{1,0:T(4,128)S(1)}, f32[4,512]{1,0:T(4,128)}, u32[]{:S(2)}) copy-start(f32[4,512]{1,0:T(4,128)} %param.16) | copy-start | bytes 24580
  354.0 5.0 %copy-start.3 = (f32[4,512,128]{1,2,0:T(8,128)S(1)}, f32[4,512,128]{1,2,0:T(8,128)}, u32[]{:S(2)}) copy-start(f32[4,512,128]{1,2,0:T(8,128)} %copy-done.2) | copy-start | bytes 3145732
